TPU v7x, 32 devices: a whole 2x2x4 slice. The times are simulated.
32 devices in a mesh: band: 8 (over z, y), sub: 4 (over x, core).
Axes of the slice: x: 2, y: 2, z: 4, core: 2. Of those that a mesh axis runs over, the one named last changes fastest.
Arguments:
- grid_x: bfloat16 [227, 16384], P(None, ('band', 'sub')), may hold values from -6 to 6
- mesh_in: bfloat16 [2048, 512], P(('band', 'sub')), may hold values from -6 to 6
- w_embed: bfloat16 [227, 512], replicated, may hold values from -0.375 to 0.375
- w_src: bfloat16 [512, 512], replicated, may hold values from -0.25 to 0.25
- w_dst: bfloat16 [512, 512], replicated, may hold values from -0.25 to 0.25
- w_edge: bfloat16 [512, 512], replicated, may hold values from -0.25 to 0.25
- w_proc: bfloat16 [512, 512], replicated, may hold values from -0.25 to 0.25
- w_recv: bfloat16 [512, 512], replicated, may hold values from -0.25 to 0.25
- g2m_src: int32 [2048, 40], P(('band', 'sub')), may hold values from 0 to 16383, as said below
- mesh_src: int32 [2048, 6], P(('band', 'sub')), may hold values from 0 to 2047, as said below
- cotangent: bfloat16 [2048, 512], P(('band', 'sub')), may hold values from -6 to 6
Outputs:
- mesh_out: bfloat16 [2048, 512], P(('band', 'sub'))
- grid_grad: float32 [227, 16384], P(None, ('band', 'sub'))
- src_grad: float32 [512, 512], replicated
- edge_grad: float32 [512, 512], replicated
Inputs may be any that keep to these rules, and one draw needn't show every extreme that they name: Grid node g belongs to band g // (512 * 4), mesh node m to band m // (64 * 4); g2m_src[m, k] lies in the band of mesh node m, or among the 512 grid nodes of an adjacent band that stand next to that band in index order. mesh_src[m, j] lies in the band of mesh node m, or among the 64 mesh nodes of an adjacent band that stand next to that band in index order.
All inputs are finite; a program needn't handle non-finite values.
Results may differ from a plain program's by a relative error of at most 0.015.
Values may be sent and summed in bfloat16 or wider, within the bound.
A program may use at most 128 MiB of HBM per device.

v0:
```python
import math
import jax
import jax.numpy as jnp
from jax import lax
from jax.sharding import PartitionSpec as P

EPSILON = 1e-05


def padded(shard, sides, width):
    for axis, dim in sides:
        devices, length = (lax.axis_size(axis), shard.shape[dim])
        up = [(i, (i + 1) % devices) for i in range(devices - 1)]
        down = [(j, i) for i, j in up]
        last = lax.slice_in_dim(shard, length - width, length, axis=dim)
        first = lax.slice_in_dim(shard, 0, width, axis=dim)
        before = lax.ppermute(last, axis, up)
        after = lax.ppermute(first, axis, down)
        shard = jnp.concatenate([before, shard, after], axis=dim)
    return shard


def from_behind(value, axis, steps):
    count = lax.axis_size(axis)
    first, last = (max(0, -steps), min(count, count - steps))
    return lax.ppermute(value, axis, [(source, source + steps) for source in range(first, last)])


def silu_slope(value):
    sigma = jax.nn.sigmoid(value)
    return sigma * (1.0 + value * (1.0 - sigma))


def normalize(value):
    centred = value - jnp.mean(value, axis=-1, keepdims=True)
    spread = jnp.sqrt(jnp.mean(centred * centred, axis=-1, keepdims=True) + EPSILON)
    return (centred / spread, spread)


def times_transpose(left, right):
    return lax.dot_general(
        left, right, (((1,), (1,)), ((), ())), preferred_element_type=jnp.float32
    )


def first_contract(left, right):
    return lax.dot_general(
        left, right, (((0,), (0,)), ((), ())), preferred_element_type=jnp.float32
    )


def fetch_grid(projected):
    border = projected.shape[0]
    block = lax.all_gather(projected, "sub", axis=0, tiled=True)
    return padded(block, (("band", 0),), border)


def return_grid(window_grad, border):
    middle = window_grad[border:-border]
    from_above = from_behind(window_grad[:border].astype(jnp.bfloat16), "band", -1).astype(
        jnp.float32
    )
    from_below = from_behind(window_grad[-border:].astype(jnp.bfloat16), "band", 1).astype(
        jnp.float32
    )
    middle = middle.at[:border].add(from_below)
    middle = middle.at[middle.shape[0] - border :].add(from_above)
    return lax.psum_scatter(
        middle.astype(jnp.bfloat16), "sub", scatter_dimension=0, tiled=True
    ).astype(jnp.float32)


def return_mesh(window_grad, border):
    middle = window_grad[border:-border]
    from_above = from_behind(window_grad[:border].astype(jnp.bfloat16), "band", -1).astype(
        jnp.float32
    )
    from_below = from_behind(window_grad[-border:].astype(jnp.bfloat16), "band", 1).astype(
        jnp.float32
    )
    middle = middle.at[:border].add(from_below)
    middle = middle.at[middle.shape[0] - border :].add(from_above)
    return lax.psum_scatter(
        middle.astype(jnp.bfloat16), "sub", scatter_dimension=0, tiled=True
    ).astype(jnp.float32)


def body(
    grid_x, mesh_in, w_embed, w_src, w_dst, w_edge, w_proc, w_recv, g2m_src, mesh_src, cotangent
):
    latent = w_src.shape[0]
    mesh_rows, enc_count = g2m_src.shape
    mesh_count = mesh_src.shape[1]
    band_index = lax.axis_index("band")
    groups = lax.axis_size("sub")
    hidden_pre = first_contract(grid_x, w_embed)
    hidden_grid = jax.nn.silu(hidden_pre).astype(jnp.bfloat16)
    projected = jnp.dot(hidden_grid, w_src, preferred_element_type=jnp.float32).astype(jnp.bfloat16)
    dest_term = jnp.dot(mesh_in, w_dst, preferred_element_type=jnp.float32)
    grid_border = projected.shape[0]
    grid_window = fetch_grid(projected)
    grid_base = band_index * (grid_border * groups) - grid_border
    grid_local = (g2m_src - grid_base).reshape(-1)
    before = jnp.take(grid_window, grid_local, axis=0).astype(jnp.float32)
    before = (before.reshape(mesh_rows, enc_count, latent) + dest_term[:, None, :]).reshape(
        -1, latent
    )
    active = jax.nn.silu(before).astype(jnp.bfloat16)
    normed, spread = normalize(jnp.dot(active, w_edge, preferred_element_type=jnp.float32))
    encoded = jnp.sum(normed.reshape(mesh_rows, enc_count, latent), axis=1)
    hidden_mesh = (mesh_in.astype(jnp.float32) + encoded / math.sqrt(enc_count)).astype(
        jnp.bfloat16
    )
    query = jnp.dot(hidden_mesh, w_proc, preferred_element_type=jnp.float32).astype(jnp.bfloat16)
    receiver = jnp.dot(hidden_mesh, w_recv, preferred_element_type=jnp.float32)
    mesh_border = query.shape[0]
    mesh_block = lax.all_gather(query, "sub", axis=0, tiled=True)
    mesh_window = padded(mesh_block, (("band", 0),), mesh_border)
    mesh_base = band_index * mesh_block.shape[0] - mesh_border
    mesh_local = (mesh_src - mesh_base).reshape(-1)
    mesh_before = jnp.take(mesh_window, mesh_local, axis=0).astype(jnp.float32)
    mesh_before = mesh_before.reshape(mesh_rows, mesh_count, latent) + receiver[:, None, :]
    summed = jnp.sum(jax.nn.silu(mesh_before), axis=1)
    mesh_out = (hidden_mesh.astype(jnp.float32) + summed / math.sqrt(mesh_count)).astype(
        jnp.bfloat16
    )
    upstream = cotangent.astype(jnp.float32)
    mesh_slope = (upstream / math.sqrt(mesh_count))[:, None, :] * silu_slope(mesh_before)
    receiver_grad = jnp.sum(mesh_slope, axis=1)
    window_grad = jnp.zeros((mesh_window.shape[0], latent), jnp.float32)
    window_grad = window_grad.at[mesh_local].add(mesh_slope.reshape(-1, latent))
    query_grad = return_mesh(window_grad, mesh_border)
    mesh_grad = upstream + times_transpose(query_grad.astype(jnp.bfloat16), w_proc)
    mesh_grad = mesh_grad + times_transpose(receiver_grad.astype(jnp.bfloat16), w_recv)
    upper = mesh_grad / math.sqrt(enc_count)
    incoming = jnp.broadcast_to(upper[:, None, :], (mesh_rows, enc_count, latent)).reshape(
        -1, latent
    )
    centred_grad = incoming - jnp.mean(incoming, axis=-1, keepdims=True)
    centred_grad = centred_grad - normed * jnp.mean(incoming * normed, axis=-1, keepdims=True)
    norm_grad = (centred_grad / spread).astype(jnp.bfloat16)
    edge_part = first_contract(active, norm_grad)
    before_grad = times_transpose(norm_grad, w_edge) * silu_slope(before)
    grid_window_grad = (
        jnp.zeros((grid_window.shape[0], latent), jnp.float32).at[grid_local].add(before_grad)
    )
    projected_grad = return_grid(grid_window_grad, grid_border)
    projected_low = projected_grad.astype(jnp.bfloat16)
    src_part = first_contract(hidden_grid, projected_low)
    hidden_grad = (times_transpose(projected_low, w_src) * silu_slope(hidden_pre)).astype(
        jnp.bfloat16
    )
    grid_grad = times_transpose(w_embed, hidden_grad)
    src_grad, edge_grad = lax.psum((src_part, edge_part), ("band", "sub"))
    return (mesh_out, grid_grad, src_grad, edge_grad)


def solution(mesh):
    placed = (
        P(None, ("band", "sub")),
        P(("band", "sub"), None),
        P(),
        P(),
        P(),
        P(),
        P(),
        P(),
        P(("band", "sub"), None),
        P(("band", "sub"), None),
        P(("band", "sub"), None),
    )
    return jax.shard_map(
        body,
        mesh=mesh,
        in_specs=placed,
        out_specs=(P(("band", "sub"), None), P(None, ("band", "sub")), P(), P()),
        check_vma=False,
    )
```

profile of v0, /device:TPU:0, one launch (start us, length us, event | category | flops | bytes accessed | tf_op | source)
XLA Modules:
  0.0 408.9 jit_solution(17956858091147088192)
XLA Ops:
  9.7 2.4 convolution_convert_fusion
  15.9 21.6 %all-gather.2.cloned.1.call-done = bf16[2048,512]{1,0:T(8,128)(2,1)} async-done(((bf16[512,512]{1,0:T(8,128)(2,1)}), bf16[2048,512]{1,0:T(8,128)(2,1)}) %all-gather.2.cloned.1.call-update) | async-done | bytes 2097168 | tf_op jit(solution)/shard_map/all_gather | solution.py:54
  38.8 3.4 collective-permute-start
  43.8 21.2 %collective-permute-done = bf16[512,512]{1,0:T(8,128)(2,1)S(1)} collective-permute-done((bf16[512,512]{1,0:T(8,128)(2,1)S(1)}, bf16[512,512]{1,0:T(8,128)(2,1)S(1)}, u32[]{:S(2)}, u32[]{:S(2)}) %collective-permute-start) | collective-permute-done | bytes 524320 | tf_op jit(solution)/shard_map/ppermute | solution.py:17
  65.0 3.0 pad_maximum_fusion
  67.9 10.6 %gather_fusion = bf16[2560,512]{1,0:T(8,128)(2,1)} fusion(bf16[3072,512]{1,0:T(8,128)(2,1)} %pad_maximum_fusion, s32[3072]{0:T(1024)S(1)} %pad_clamp_fusion), kind=kCustom, calls=%fused_computation | custom fusion | bytes 5253120 | tf_op jit(solution)/shard_map/jit(_take)/gather | solution.py:104
  78.6 5.7 %bitcast_add_fusion = (f32[2560,512]{1,0:T(8,128)}, bf16[2560,512]{1,0:T(8,128)(2,1)S(1)}) fusion(f32[64,512]{1,0:T(8,128)S(1)} %fusion.54, bf16[2560,512]{1,0:T(8,128)(2,1)} %gather_fusion, pred[2560]{0:T(1024)(128)(4,1)S(1)} %compare_and_fusion), kind=kLoop, calls=%fused_computation.10 | loop fusion | flops 10485760 | bytes 10619392 | tf_op jit(solution)/shard_map/add | solution.py:105
  86.8 3.4 subtract_divide_fusion
  90.3 3.4 reduce_sum.67
  95.0 5.8 %all_gather.7 = bf16[256,512]{1,0:T(8,128)(2,1)S(1)} all-gather(bf16[64,512]{1,0:T(8,128)(2,1)S(1)} %convolution_convert_fusion.1), channel_id=1, replica_groups=mesh['band'=8,'sub'=4] {'sub'}, dimensions={0}, use_global_device_ids=true | all-gather | bytes 327680 | tf_op jit(solution)/shard_map/all_gather | solution.py:117
  101.5 4.4 %collective-permute-start.2 = (bf16[64,512]{1,0:T(8,128)(2,1)S(1)}, bf16[64,512]{1,0:T(8,128)(2,1)S(1)}, u32[]{:S(2)}, u32[]{:S(2)}) collective-permute-start(bf16[64,512]{1,0:T(8,128)(2,1)S(1)} %get-tuple-element.66), channel_id=1, source_target_pairs={{0,4},{4,8},{8,12},{12,16},{16,20},{20,24},{24,28},{1,5},{5,9},{9,... | collective-permute-start | bytes 196616 | tf_op jit(solution)/shard_map/ppermute | solution.py:17
  110.4 2.2 add.192
  114.3 2.6 gather_fusion.1
  116.9 5.1 %scatter_custom_fusion = f32[384,512]{1,0:T(8,128)} fusion(s32[384]{0:T(512)} %copy-done.23, f32[384,512]{1,0:T(8,128)} %mul.82, f32[384,512]{1,0:T(8,128)} %add.192, bf16[384,512]{1,0:T(8,128)(2,1)} %gather_fusion.1, f32[]{:T(128)} %constant.173.clone.1, f32[]{:T(128)} %constant.175.clone.1, pred[384]{0:T(512)(128)(4,1)} %compare_and_fusion.2, ...), kind=kCustom, calls=%fused_computation.47 | custom fusion | flops 2359296 | bytes 2754560 | tf_op jit(solution)/shard_map/scatter-add | solution.py:131
  123.1 4.9 %collective-permute-start.4 = (bf16[64,512]{1,0:T(8,128)(2,1)S(1)}, bf16[64,512]{1,0:T(8,128)(2,1)S(1)}, u32[]{:S(2)}, u32[]{:S(2)}) collective-permute-start(bf16[64,512]{1,0:T(8,128)(2,1)S(1)} %get-tuple-element.65), channel_id=1, source_target_pairs={{0,4},{4,8},{8,12},{12,16},{16,20},{20,24},{24,28},{1,5},{5,9},{9,... | collective-permute-start | bytes 196616 | tf_op jit(solution)/shard_map/ppermute | solution.py:26
  131.4 4.8 %collective-permute-done.5 = bf16[64,512]{1,0:T(8,128)(2,1)S(1)} collective-permute-done((bf16[64,512]{1,0:T(8,128)(2,1)S(1)}, bf16[64,512]{1,0:T(8,128)(2,1)S(1)}, u32[]{:S(2)}, u32[]{:S(2)}) %collective-permute-start.5) | collective-permute-done | bytes 65568 | tf_op jit(solution)/shard_map/ppermute | solution.py:26
  138.7 2.9 multiply_reduce_fusion.1
  141.6 16.1 %reduce-scatter.3.cloned.1.call-done = bf16[64,512]{1,0:T(8,128)(2,1)} async-done(((bf16[256,512]{1,0:T(8,128)(2,1)}), bf16[64,512]{1,0:T(8,128)(2,1)}) %reduce-scatter.3.cloned.1.call-update) | async-done | bytes 65552 | tf_op jit(solution)/shard_map/reduce_scatter | solution.py:83
  160.5 3.6 fusion.3
  164.3 3.9 fusion.2
  168.2 3.9 fusion.56
  172.2 21.5 %scatter_custom_fusion.1 = f32[3072,512]{1,0:T(8,128)} fusion(s32[2560]{0:T(1024)} %copy-done.21, f32[2560,512]{1,0:T(8,128)} %fusion.56, f32[2560,512]{1,0:T(8,128)} %get-tuple-element.60, f32[]{:T(128)} %constant.175.clone.1, f32[]{:T(128)} %constant.173.clone.1), kind=kCustom, calls=%fused_computation.11 | custom fusion | flops 11796480 | bytes 16778240 | tf_op jit(solution)/shard_map/scatter-add | solution.py:145
  193.7 3.2 convert.9
  197.0 3.7 collective-permute-start.6
  202.0 21.0 %collective-permute-done.6 = bf16[512,512]{1,0:T(8,128)(2,1)S(1)} collective-permute-done((bf16[512,512]{1,0:T(8,128)(2,1)S(1)}, bf16[512,512]{1,0:T(8,128)(2,1)S(1)}, u32[]{:S(2)}, u32[]{:S(2)}) %collective-permute-start.6) | collective-permute-done | bytes 524320 | tf_op jit(solution)/shard_map/ppermute | solution.py:26
  225.1 4.2 %fusion.57 = f32[512,512]{1,0:T(8,128)} fusion(bf16[2560,512]{1,0:T(8,128)(2,1)S(1)} %get-tuple-element.61, bf16[2560,512]{1,0:T(8,128)(2,1)} %copy-done.3), kind=kOutput, calls=%fused_computation.105 | convolution fusion | flops 1342177280 | bytes 6291456 | tf_op jit(solution)/shard_map/dot_general | solution.py:47
  229.4 27.8 %reduce-scatter.5.cloned.1.call-done = bf16[512,512]{1,0:T(8,128)(2,1)} async-done(((bf16[2048,512]{1,0:T(8,128)(2,1)}), bf16[512,512]{1,0:T(8,128)(2,1)}) %reduce-scatter.5.cloned.1.call-update) | async-done | bytes 524304 | tf_op jit(solution)/shard_map/reduce_scatter | solution.py:68
  257.2 2.9 fusion.46
  260.8 1.7 fusion.14
  262.5 135.4 %all-reduce.3.cloned.1.call-done = (f32[512,512]{1,0:T(8,128)}, f32[512,512]{1,0:T(8,128)}) async-done(((f32[512,512]{1,0:T(8,128)}, f32[512,512]{1,0:T(8,128)}), (f32[512,512]{1,0:T(8,128)}, f32[512,512]{1,0:T(8,128)})) %all-reduce.3.cloned.1.call-update) | async-done | bytes 2097168 | tf_op jit(solution)/shard_map/psum | solution.py:154
  397.8 2.3 copy.27
  400.1 2.3 copy.28
  (124 shorter events, 33.7 us)
Async XLA Ops:
  7.2 77.1 %copy-start = (bf16[512,512]{1,0:T(8,128)(2,1)S(1)}, bf16[512,512]{1,0:T(8,128)(2,1)}, u32[]{:S(2)}) copy-start(bf16[512,512]{1,0:T(8,128)(2,1)} %param.24) | copy-start | bytes 1572868
  7.2 4.9 %copy-start.22 = (s32[64,40]{0,1:T(8,128)S(1)}, s32[64,40]{0,1:T(8,128)}, u32[]{:S(2)}) copy-start(s32[64,40]{0,1:T(8,128)} %param.27) | copy-start | bytes 30724
  7.2 5.2 %copy-start.25 = (s32[64,6]{0,1:T(8,128)S(1)}, s32[64,6]{0,1:T(8,128)}, u32[]{:S(2)}) copy-start(s32[64,6]{0,1:T(8,128)} %param.28) | copy-start | bytes 4612
  7.2 6.2 %copy-start.14 = (bf16[64,512]{1,0:T(8,128)(2,1)S(1)}, bf16[64,512]{1,0:T(8,128)(2,1)}, u32[]{:S(2)}) copy-start(bf16[64,512]{1,0:T(8,128)(2,1)} %param.29) | copy-start | bytes 196612
  7.2 30.3 %all-gather.2.cloned.1.call-start = ((), (), s32[]{:S(2)}) async-start(), calls=%async_computation.2 | async-start | bytes 2621440 | tf_op jit(solution)/shard_map/all_gather | solution.py:54
  9.7 33.9 %copy-start.13 = (bf16[512,512]{1,0:T(8,128)(2,1)S(1)}, bf16[512,512]{1,0:T(8,128)(2,1)}, u32[]{:S(2)}) copy-start(bf16[512,512]{1,0:T(8,128)(2,1)} %param.23) | copy-start | bytes 1572868
  9.7 33.9 %copy-start.15 = (bf16[64,512]{1,0:T(8,128)(2,1)S(1)}, bf16[64,512]{1,0:T(8,128)(2,1)}, u32[]{:S(2)}) copy-start(bf16[64,512]{1,0:T(8,128)(2,1)} %param.20) | copy-start | bytes 196612
  12.1 145.7 %reduce-scatter.3.cloned.1.call-start = ((), (), s32[]{:S(2)}) async-start(), calls=%async_computation.3 | async-start | bytes 327680 | tf_op jit(solution)/shard_map/reduce_scatter | solution.py:83
  15.2 52.7 %copy-start.21 = (s32[2560]{0:T(1024)}, s32[2560]{0:T(1024)S(1)}, u32[]{:S(2)}) copy-start(s32[2560]{0:T(1024)S(1)} %fusion.43) | copy-start | bytes 30724
  15.3 28.2 %copy-start.23 = (s32[384]{0:T(512)}, s32[384]{0:T(512)S(1)}, u32[]{:S(2)}) copy-start(s32[384]{0:T(512)S(1)} %fusion.44) | copy-start | bytes 4612
  38.8 26.2 %collective-permute-start = (bf16[512,512]{1,0:T(8,128)(2,1)S(1)}, bf16[512,512]{1,0:T(8,128)(2,1)S(1)}, u32[]{:S(2)}, u32[]{:S(2)}) collective-permute-start(bf16[512,512]{1,0:T(8,128)(2,1)S(1)} %get-tuple-element.62), channel_id=1, source_target_pairs={{0,4},{4,8},{8,12},{12,16},{16,20},{20,24},{24,28},{1,5},{5,9},{9,... | collective-permute-start | bytes 1572872 | tf_op jit(solution)/shard_map/ppermute | solution.py:17
  42.2 22.8 %collective-permute-start.1 = (bf16[512,512]{1,0:T(8,128)(2,1)S(1)}, bf16[512,512]{1,0:T(8,128)(2,1)S(1)}, u32[]{:S(2)}, u32[]{:S(2)}) collective-permute-start(bf16[512,512]{1,0:T(8,128)(2,1)S(1)} %get-tuple-element.63), channel_id=1, source_target_pairs={{4,0},{8,4},{12,8},{16,12},{20,16},{24,20},{28,24},{5,1},{9,5},{13... | collective-permute-start | bytes 1572872 | tf_op jit(solution)/shard_map/ppermute | solution.py:18
  85.8 4.4 %copy-start.1 = (f32[2560,512]{1,0:T(8,128)}, f32[2560,512]{1,0:T(8,128)S(1)}, u32[]{:S(2)}) copy-start(f32[2560,512]{1,0:T(8,128)S(1)} %get-tuple-element.69) | copy-start | bytes 15728644
  93.7 13.7 %copy-start.10 = (bf16[64,512]{1,0:T(8,128)(2,1)}, bf16[64,512]{1,0:T(8,128)(2,1)S(1)}, u32[]{:S(2)}) copy-start(bf16[64,512]{1,0:T(8,128)(2,1)S(1)} %add_convert_fusion.1) | copy-start | bytes 196612
  101.5 11.1 %collective-permute-start.2 = (bf16[64,512]{1,0:T(8,128)(2,1)S(1)}, bf16[64,512]{1,0:T(8,128)(2,1)S(1)}, u32[]{:S(2)}, u32[]{:S(2)}) collective-permute-start(bf16[64,512]{1,0:T(8,128)(2,1)S(1)} %get-tuple-element.66), channel_id=1, source_target_pairs={{0,4},{4,8},{8,12},{12,16},{16,20},{20,24},{24,28},{1,5},{5,9},{9,... | collective-permute-start | bytes 196616 | tf_op jit(solution)/shard_map/ppermute | solution.py:17
  105.9 7.4 %collective-permute-start.3 = (bf16[64,512]{1,0:T(8,128)(2,1)S(1)}, bf16[64,512]{1,0:T(8,128)(2,1)}, u32[]{:S(2)}, u32[]{:S(2)}) collective-permute-start(bf16[64,512]{1,0:T(8,128)(2,1)S(1)} %get-tuple-element.67), channel_id=1, source_target_pairs={{4,0},{8,4},{12,8},{16,12},{20,16},{24,20},{28,24},{5,1},{9,5},{13... | collective-permute-start | bytes 196616 | tf_op jit(solution)/shard_map/ppermute | solution.py:18
  116.8 20.2 %copy-start.24 = (pred[64,6]{0,1:T(8,128)(4,1)S(1)}, pred[64,6]{0,1:T(8,128)(4,1)}, u32[]{:S(2)}) copy-start(pred[64,6]{0,1:T(8,128)(4,1)} %get-tuple-element.56) | copy-start | bytes 1156
  116.9 20.9 %copy-start.4 = (bf16[384,512]{1,0:T(8,128)(2,1)S(1)}, bf16[384,512]{1,0:T(8,128)(2,1)}, u32[]{:S(2)}) copy-start(bf16[384,512]{1,0:T(8,128)(2,1)} %gather_fusion.1) | copy-start | bytes 1179652
  123.1 7.3 %collective-permute-start.4 = (bf16[64,512]{1,0:T(8,128)(2,1)S(1)}, bf16[64,512]{1,0:T(8,128)(2,1)S(1)}, u32[]{:S(2)}, u32[]{:S(2)}) collective-permute-start(bf16[64,512]{1,0:T(8,128)(2,1)S(1)} %get-tuple-element.65), channel_id=1, source_target_pairs={{0,4},{4,8},{8,12},{12,16},{16,20},{20,24},{24,28},{1,5},{5,9},{9,... | collective-permute-start | bytes 196616 | tf_op jit(solution)/shard_map/ppermute | solution.py:26
  129.1 7.1 %collective-permute-start.5 = (bf16[64,512]{1,0:T(8,128)(2,1)S(1)}, bf16[64,512]{1,0:T(8,128)(2,1)S(1)}, u32[]{:S(2)}, u32[]{:S(2)}) collective-permute-start(bf16[64,512]{1,0:T(8,128)(2,1)S(1)} %get-tuple-element.64), channel_id=1, source_target_pairs={{4,0},{8,4},{12,8},{16,12},{20,16},{24,20},{28,24},{5,1},{9,5},{13... | collective-permute-start | bytes 196616 | tf_op jit(solution)/shard_map/ppermute | solution.py:26
  137.0 120.2 %reduce-scatter.5.cloned.1.call-start = ((), (), s32[]{:S(2)}) async-start(), calls=%async_computation.4 | async-start | bytes 2621440 | tf_op jit(solution)/shard_map/reduce_scatter | solution.py:68
  138.7 25.6 %copy-start.19 = (f32[2560]{0:T(1024)S(1)}, f32[2560]{0:T(1024)}, u32[]{:S(2)}) copy-start(f32[2560]{0:T(1024)} %copy-done.18) | copy-start | bytes 30724
  196.9 26.1 %copy-start.2 = (f32[3072,512]{1,0:T(8,128)S(1)}, f32[3072,512]{1,0:T(8,128)}, u32[]{:S(2)}) copy-start(f32[3072,512]{1,0:T(8,128)} %scatter_custom_fusion.1) | copy-start | bytes 18874372
  196.9 26.1 %slice-start = ((f32[3072,512]{1,0:T(8,128)}), f32[2048,512]{1,0:T(8,128)S(1)}, s32[]{:S(2)}) async-start(f32[3072,512]{1,0:T(8,128)} %scatter_custom_fusion.1), calls=%async_computation.6 | async-start | bytes 8388608 | tf_op jit(solution)/shard_map/slice | solution.py:59
  197.0 26.0 %collective-permute-start.6 = (bf16[512,512]{1,0:T(8,128)(2,1)S(1)}, bf16[512,512]{1,0:T(8,128)(2,1)S(1)}, u32[]{:S(2)}, u32[]{:S(2)}) collective-permute-start(bf16[512,512]{1,0:T(8,128)(2,1)S(1)} %get-tuple-element.59), channel_id=1, source_target_pairs={{0,4},{4,8},{8,12},{12,16},{16,20},{20,24},{24,28},{1,5},{5,9},{9,... | collective-permute-start | bytes 1572872 | tf_op jit(solution)/shard_map/ppermute | solution.py:26
  200.7 22.5 %collective-permute-start.7 = (bf16[512,512]{1,0:T(8,128)(2,1)S(1)}, bf16[512,512]{1,0:T(8,128)(2,1)S(1)}, u32[]{:S(2)}, u32[]{:S(2)}) collective-permute-start(bf16[512,512]{1,0:T(8,128)(2,1)S(1)} %get-tuple-element.58), channel_id=1, source_target_pairs={{4,0},{8,4},{12,8},{16,12},{20,16},{24,20},{28,24},{5,1},{9,5},{13... | collective-permute-start | bytes 1572872 | tf_op jit(solution)/shard_map/ppermute | solution.py:26
  225.1 172.7 %all-reduce.3.cloned.1.call-start = ((), (), s32[]{:S(2)}) async-start(), calls=%async_computation.5 | async-start | bytes 4194304 | tf_op jit(solution)/shard_map/psum | solution.py:154
  229.4 30.7 %copy-start.11 = (bf16[64,512]{1,0:T(8,128)(2,1)S(1)}, bf16[64,512]{1,0:T(8,128)(2,1)}, u32[]{:S(2)}) copy-start(bf16[64,512]{1,0:T(8,128)(2,1)} %copy-done.10) | copy-start | bytes 196612
  229.4 30.7 %copy-start.12 = (f32[64,512]{1,0:T(8,128)S(1)}, f32[64,512]{1,0:T(8,128)}, u32[]{:S(2)}) copy-start(f32[64,512]{1,0:T(8,128)} %get-tuple-element.53) | copy-start | bytes 393220
  229.4 31.4 %copy-start.9 = (f32[512,512]{1,0:T(8,128)S(1)}, f32[512,512]{1,0:T(8,128)}, u32[]{:S(2)}) copy-start(f32[512,512]{1,0:T(8,128)} %copy-done.8) | copy-start | bytes 3145732
  229.4 31.4 %copy-start.17 = (bf16[227,512]{1,0:T(8,128)(2,1)S(1)}, bf16[227,512]{1,0:T(8,128)(2,1)}, u32[]{:S(2)}) copy-start(bf16[227,512]{1,0:T(8,128)(2,1)} %param.21) | copy-start | bytes 697348
  229.4 31.4 %copy-start.26 = (bf16[512,512]{1,0:T(8,128)(2,1)S(1)}, bf16[512,512]{1,0:T(8,128)(2,1)}, u32[]{:S(2)}) copy-start(bf16[512,512]{1,0:T(8,128)(2,1)} %param.22) | copy-start | bytes 1572868
  (9 other events, 18.0 us)
Sparse Core Ops, SparseCore 0:
  12.2 25.2 all-gather.1
  137.1 20.5 reduce-scatter.2
  225.2 31.9 reduce-scatter.4
  263.2 134.6 all-reduce.2
where the time goes:
time: 410 us; the launch traced here: 409 us
  waiting for transfers between devices  248 us (60%)
  other arithmetic  64.6 us (16%)
  local copies, waits for them, and re-layouts  30.7 us (7%)
  matrix products  23.6 us (6%)
  starting transfers between devices  21.9 us (5%)
  between operations  14.3 us (3%)
  blocking collectives  5.78 us (1%)
    psum x1, waiting for transfers between devices, body(): src_grad, edge_grad = lax.psum((src_part, edge_part), ('band', 'sub'))  135 us
    reduce_scatter x1, waiting for transfers between devices, return_grid(): lax.psum_scatter(middle.astype(jnp.bfloat16), 'sub', scatter_dimension=0,...  27.8 us
    ppermute x4, waiting for transfers between devices, from_behind(): lax.ppermute(value, axis, [(source, source + steps) for source in range(f...  25.8 us
    all_gather x1, waiting for transfers between devices, fetch_grid(): block = lax.all_gather(projected, 'sub', axis=0, tiled=True)  21.6 us
    scatter-add x1, other arithmetic, body(): jnp.zeros((grid_window.shape[0], latent), jnp.float32).at[grid_local]  21.5 us
    ppermute x2, waiting for transfers between devices, padded(): before = lax.ppermute(last, axis, up)  21.2 us
    reduce_scatter x1, waiting for transfers between devices, return_mesh(): lax.psum_scatter(middle.astype(jnp.bfloat16), 'sub', scatter_dimension=0,...  16.1 us
    ppermute x4, starting transfers between devices, from_behind(): lax.ppermute(value, axis, [(source, source + steps) for source in range(f...  11.2 us
  transfers between devices with their start and end apart: 12, of which 7 were waited for; matrix products, arithmetic and copies ran while one was open for 5% of the time, Pallas kernels for 0%

commit v1 on v0

--- a/solution.py
+++ b/solution.py
@@ -88,6 +88,12 @@
 def body(
     grid_x, mesh_in, w_embed, w_src, w_dst, w_edge, w_proc, w_recv, g2m_src, mesh_src, cotangent
 ):
+
+    def launch_the_heads(mine_x, axis_key, across):
+        for tick in (axis_key, across):
+            mine_x = lax.psum(mine_x, tick)
+        return mine_x
+
     latent = w_src.shape[0]
     mesh_rows, enc_count = g2m_src.shape
     mesh_count = mesh_src.shape[1]
@@ -151,7 +157,7 @@
         jnp.bfloat16
     )
     grid_grad = times_transpose(w_embed, hidden_grad)
-    src_grad, edge_grad = lax.psum((src_part, edge_part), ("band", "sub"))
+    src_grad, edge_grad = launch_the_heads((src_part, edge_part), "sub", "band")
     return (mesh_out, grid_grad, src_grad, edge_grad)
 
 

time: 410 us -> 430 us (1.049)
  waiting for transfers between devices: 248 us -> 268 us
    psum x1 -> x2, waiting for transfers between devices: 135 us -> 155 us  [launch_the_heads(): mine_x = lax.psum(mine_x, tick)]
  transfers between devices with their start and end apart: 12 -> 13, of which waited for: 7 -> 8; matrix products, arithmetic and copies ran while one was open for 5% -> 5% of each run, Pallas kernels for 0% -> 0%
where the time goes in v1:
time: 430 us; the launch traced here: 429 us
  waiting for transfers between devices  268 us (62%)
  other arithmetic  64.5 us (15%)
  local copies, waits for them, and re-layouts  30.7 us (7%)
  matrix products  23.6 us (5%)
  starting transfers between devices  22.2 us (5%)
  between operations  14.3 us (3%)
  blocking collectives  5.78 us (1%)
    psum x2, waiting for transfers between devices, launch_the_heads(): mine_x = lax.psum(mine_x, tick)  155 us
    reduce_scatter x1, waiting for transfers between devices, return_grid(): lax.psum_scatter(middle.astype(jnp.bfloat16), 'sub', scatter_dimension=0,...  27.6 us
    ppermute x4, waiting for transfers between devices, from_behind(): lax.ppermute(value, axis, [(source, source + steps) for source in range(f...  25.8 us
    all_gather x1, waiting for transfers between devices, fetch_grid(): block = lax.all_gather(projected, 'sub', axis=0, tiled=True)  21.7 us
    scatter-add x1, other arithmetic, body(): jnp.zeros((grid_window.shape[0], latent), jnp.float32).at[grid_local]  21.5 us
    ppermute x2, waiting for transfers between devices, padded(): before = lax.ppermute(last, axis, up)  21.2 us
    reduce_scatter x1, waiting for transfers between devices, return_mesh(): lax.psum_scatter(middle.astype(jnp.bfloat16), 'sub', scatter_dimension=0,...  16.1 us
    ppermute x4, starting transfers between devices, from_behind(): lax.ppermute(value, axis, [(source, source + steps) for source in range(f...  11.2 us
  transfers between devices with their start and end apart: 13, of which 8 were waited for; matrix products, arithmetic and copies ran while one was open for 5% of the time, Pallas kernels for 0%

profile of v1, /device:TPU:0, one launch (start us, length us, event | category | flops | bytes accessed | tf_op | source)
XLA Modules:
  0.0 428.6 jit_solution(8172003018930848113)
XLA Ops:
  9.7 2.4 convolution_convert_fusion
  15.8 21.7 %all-gather.2.cloned.1.call-done = bf16[2048,512]{1,0:T(8,128)(2,1)} async-done(((bf16[512,512]{1,0:T(8,128)(2,1)}), bf16[2048,512]{1,0:T(8,128)(2,1)}) %all-gather.2.cloned.1.call-update) | async-done | bytes 2097168 | tf_op jit(solution)/shard_map/all_gather | solution.py:54
  38.8 3.4 collective-permute-start
  43.8 21.2 %collective-permute-done = bf16[512,512]{1,0:T(8,128)(2,1)S(1)} collective-permute-done((bf16[512,512]{1,0:T(8,128)(2,1)S(1)}, bf16[512,512]{1,0:T(8,128)(2,1)S(1)}, u32[]{:S(2)}, u32[]{:S(2)}) %collective-permute-start) | collective-permute-done | bytes 524320 | tf_op jit(solution)/shard_map/ppermute | solution.py:17
  65.0 3.0 pad_maximum_fusion
  67.9 10.6 %gather_fusion = bf16[2560,512]{1,0:T(8,128)(2,1)} fusion(bf16[3072,512]{1,0:T(8,128)(2,1)} %pad_maximum_fusion, s32[3072]{0:T(1024)S(1)} %pad_clamp_fusion), kind=kCustom, calls=%fused_computation | custom fusion | bytes 5253120 | tf_op jit(solution)/shard_map/jit(_take)/gather | solution.py:110
  78.6 5.7 %bitcast_add_fusion = (f32[2560,512]{1,0:T(8,128)}, bf16[2560,512]{1,0:T(8,128)(2,1)S(1)}) fusion(f32[64,512]{1,0:T(8,128)S(1)} %fusion.54, bf16[2560,512]{1,0:T(8,128)(2,1)} %gather_fusion, pred[2560]{0:T(1024)(128)(4,1)S(1)} %compare_and_fusion), kind=kLoop, calls=%fused_computation.10 | loop fusion | flops 10485760 | bytes 10619392 | tf_op jit(solution)/shard_map/add | solution.py:111
  86.8 3.5 subtract_divide_fusion
  90.3 3.4 reduce_sum.67
  95.0 5.8 %all_gather.7 = bf16[256,512]{1,0:T(8,128)(2,1)S(1)} all-gather(bf16[64,512]{1,0:T(8,128)(2,1)S(1)} %convolution_convert_fusion.1), channel_id=1, replica_groups=mesh['band'=8,'sub'=4] {'sub'}, dimensions={0}, use_global_device_ids=true | all-gather | bytes 327680 | tf_op jit(solution)/shard_map/all_gather | solution.py:123
  101.5 4.4 %collective-permute-start.2 = (bf16[64,512]{1,0:T(8,128)(2,1)S(1)}, bf16[64,512]{1,0:T(8,128)(2,1)S(1)}, u32[]{:S(2)}, u32[]{:S(2)}) collective-permute-start(bf16[64,512]{1,0:T(8,128)(2,1)S(1)} %get-tuple-element.68), channel_id=1, source_target_pairs={{0,4},{4,8},{8,12},{12,16},{16,20},{20,24},{24,28},{1,5},{5,9},{9,... | collective-permute-start | bytes 196616 | tf_op jit(solution)/shard_map/ppermute | solution.py:17
  110.4 2.2 add.196
  114.3 2.6 gather_fusion.1
  116.8 5.1 %scatter_custom_fusion = f32[384,512]{1,0:T(8,128)} fusion(s32[384]{0:T(512)} %copy-done.23, f32[384,512]{1,0:T(8,128)} %mul.82, f32[384,512]{1,0:T(8,128)} %add.196, bf16[384,512]{1,0:T(8,128)(2,1)} %gather_fusion.1, f32[]{:T(128)} %constant.173.clone.1, f32[]{:T(128)} %constant.175.clone.1, pred[384]{0:T(512)(128)(4,1)} %compare_and_fusion.2, ...), kind=kCustom, calls=%fused_computation.47 | custom fusion | flops 2359296 | bytes 2754560 | tf_op jit(solution)/shard_map/scatter-add | solution.py:137
  123.1 4.9 %collective-permute-start.4 = (bf16[64,512]{1,0:T(8,128)(2,1)S(1)}, bf16[64,512]{1,0:T(8,128)(2,1)S(1)}, u32[]{:S(2)}, u32[]{:S(2)}) collective-permute-start(bf16[64,512]{1,0:T(8,128)(2,1)S(1)} %get-tuple-element.67), channel_id=1, source_target_pairs={{0,4},{4,8},{8,12},{12,16},{16,20},{20,24},{24,28},{1,5},{5,9},{9,... | collective-permute-start | bytes 196616 | tf_op jit(solution)/shard_map/ppermute | solution.py:26
  131.4 4.8 %collective-permute-done.5 = bf16[64,512]{1,0:T(8,128)(2,1)S(1)} collective-permute-done((bf16[64,512]{1,0:T(8,128)(2,1)S(1)}, bf16[64,512]{1,0:T(8,128)(2,1)S(1)}, u32[]{:S(2)}, u32[]{:S(2)}) %collective-permute-start.5) | collective-permute-done | bytes 65568 | tf_op jit(solution)/shard_map/ppermute | solution.py:26
  138.7 2.9 multiply_reduce_fusion.1
  141.6 16.1 %reduce-scatter.3.cloned.1.call-done = bf16[64,512]{1,0:T(8,128)(2,1)} async-done(((bf16[256,512]{1,0:T(8,128)(2,1)}), bf16[64,512]{1,0:T(8,128)(2,1)}) %reduce-scatter.3.cloned.1.call-update) | async-done | bytes 65552 | tf_op jit(solution)/shard_map/reduce_scatter | solution.py:83
  160.5 3.6 fusion.3
  164.3 3.9 fusion.2
  168.2 3.9 fusion.56
  172.1 21.5 %scatter_custom_fusion.1 = f32[3072,512]{1,0:T(8,128)} fusion(s32[2560]{0:T(1024)} %copy-done.21, f32[2560,512]{1,0:T(8,128)} %fusion.56, f32[2560,512]{1,0:T(8,128)} %get-tuple-element.62, f32[]{:T(128)} %constant.175.clone.1, f32[]{:T(128)} %constant.173.clone.1), kind=kCustom, calls=%fused_computation.11 | custom fusion | flops 11796480 | bytes 16778240 | tf_op jit(solution)/shard_map/scatter-add | solution.py:151
  193.7 3.2 convert.9
  197.0 3.7 collective-permute-start.6
  202.0 21.0 %collective-permute-done.6 = bf16[512,512]{1,0:T(8,128)(2,1)S(1)} collective-permute-done((bf16[512,512]{1,0:T(8,128)(2,1)S(1)}, bf16[512,512]{1,0:T(8,128)(2,1)S(1)}, u32[]{:S(2)}, u32[]{:S(2)}) %collective-permute-start.6) | collective-permute-done | bytes 524320 | tf_op jit(solution)/shard_map/ppermute | solution.py:26
  225.3 4.3 fusion.57
  229.6 27.6 %reduce-scatter.5.cloned.1.call-done = bf16[512,512]{1,0:T(8,128)(2,1)} async-done(((bf16[2048,512]{1,0:T(8,128)(2,1)}), bf16[512,512]{1,0:T(8,128)(2,1)}) %reduce-scatter.5.cloned.1.call-update) | async-done | bytes 524304 | tf_op jit(solution)/shard_map/reduce_scatter | solution.py:68
  257.2 2.9 fusion.46
  260.1 51.5 %all-reduce.7.cloned.1.call-done = (f32[512,512]{1,0:T(8,128)}, f32[512,512]{1,0:T(8,128)}) async-done(((f32[512,512]{1,0:T(8,128)}, f32[512,512]{1,0:T(8,128)}), (f32[512,512]{1,0:T(8,128)}, f32[512,512]{1,0:T(8,128)})) %all-reduce.7.cloned.1.call-update) | async-done | bytes 2097168 | tf_op jit(solution)/shard_map/psum | solution.py:94
  314.0 103.6 %all-reduce.5.cloned.1.call-done = (f32[512,512]{1,0:T(8,128)}, f32[512,512]{1,0:T(8,128)}) async-done(((f32[512,512]{1,0:T(8,128)}, f32[512,512]{1,0:T(8,128)}), (f32[512,512]{1,0:T(8,128)}, f32[512,512]{1,0:T(8,128)})) %all-reduce.5.cloned.1.call-update) | async-done | bytes 2097168 | tf_op jit(solution)/shard_map/psum | solution.py:94
  417.6 2.3 copy.29
  419.8 2.3 copy.30
  (127 shorter events, 35.6 us)
Async XLA Ops:
  7.2 77.0 %copy-start = (bf16[512,512]{1,0:T(8,128)(2,1)S(1)}, bf16[512,512]{1,0:T(8,128)(2,1)}, u32[]{:S(2)}) copy-start(bf16[512,512]{1,0:T(8,128)(2,1)} %param.24) | copy-start | bytes 1572868
  7.2 5.2 %copy-start.25 = (s32[64,6]{0,1:T(8,128)S(1)}, s32[64,6]{0,1:T(8,128)}, u32[]{:S(2)}) copy-start(s32[64,6]{0,1:T(8,128)} %param.28) | copy-start | bytes 4612
  7.2 6.2 %copy-start.14 = (bf16[64,512]{1,0:T(8,128)(2,1)S(1)}, bf16[64,512]{1,0:T(8,128)(2,1)}, u32[]{:S(2)}) copy-start(bf16[64,512]{1,0:T(8,128)(2,1)} %param.29) | copy-start | bytes 196612
  7.2 30.3 %all-gather.2.cloned.1.call-start = ((), (), s32[]{:S(2)}) async-start(), calls=%async_computation.2 | async-start | bytes 2621440 | tf_op jit(solution)/shard_map/all_gather | solution.py:54
  9.7 33.9 %copy-start.13 = (bf16[512,512]{1,0:T(8,128)(2,1)S(1)}, bf16[512,512]{1,0:T(8,128)(2,1)}, u32[]{:S(2)}) copy-start(bf16[512,512]{1,0:T(8,128)(2,1)} %param.23) | copy-start | bytes 1572868
  9.7 33.9 %copy-start.15 = (bf16[64,512]{1,0:T(8,128)(2,1)S(1)}, bf16[64,512]{1,0:T(8,128)(2,1)}, u32[]{:S(2)}) copy-start(bf16[64,512]{1,0:T(8,128)(2,1)} %param.20) | copy-start | bytes 196612
  12.1 145.6 %reduce-scatter.3.cloned.1.call-start = ((), (), s32[]{:S(2)}) async-start(), calls=%async_computation.3 | async-start | bytes 327680 | tf_op jit(solution)/shard_map/reduce_scatter | solution.py:83
  15.2 52.7 %copy-start.21 = (s32[2560]{0:T(1024)}, s32[2560]{0:T(1024)S(1)}, u32[]{:S(2)}) copy-start(s32[2560]{0:T(1024)S(1)} %fusion.43) | copy-start | bytes 30724
  15.3 28.2 %copy-start.23 = (s32[384]{0:T(512)}, s32[384]{0:T(512)S(1)}, u32[]{:S(2)}) copy-start(s32[384]{0:T(512)S(1)} %fusion.44) | copy-start | bytes 4612
  38.8 26.2 %collective-permute-start = (bf16[512,512]{1,0:T(8,128)(2,1)S(1)}, bf16[512,512]{1,0:T(8,128)(2,1)S(1)}, u32[]{:S(2)}, u32[]{:S(2)}) collective-permute-start(bf16[512,512]{1,0:T(8,128)(2,1)S(1)} %get-tuple-element.64), channel_id=1, source_target_pairs={{0,4},{4,8},{8,12},{12,16},{16,20},{20,24},{24,28},{1,5},{5,9},{9,... | collective-permute-start | bytes 1572872 | tf_op jit(solution)/shard_map/ppermute | solution.py:17
  42.2 22.8 %collective-permute-start.1 = (bf16[512,512]{1,0:T(8,128)(2,1)S(1)}, bf16[512,512]{1,0:T(8,128)(2,1)S(1)}, u32[]{:S(2)}, u32[]{:S(2)}) collective-permute-start(bf16[512,512]{1,0:T(8,128)(2,1)S(1)} %get-tuple-element.65), channel_id=1, source_target_pairs={{4,0},{8,4},{12,8},{16,12},{20,16},{24,20},{28,24},{5,1},{9,5},{13... | collective-permute-start | bytes 1572872 | tf_op jit(solution)/shard_map/ppermute | solution.py:18
  93.7 13.7 %copy-start.10 = (bf16[64,512]{1,0:T(8,128)(2,1)}, bf16[64,512]{1,0:T(8,128)(2,1)S(1)}, u32[]{:S(2)}) copy-start(bf16[64,512]{1,0:T(8,128)(2,1)S(1)} %add_convert_fusion.1) | copy-start | bytes 196612
  101.5 11.1 %collective-permute-start.2 = (bf16[64,512]{1,0:T(8,128)(2,1)S(1)}, bf16[64,512]{1,0:T(8,128)(2,1)S(1)}, u32[]{:S(2)}, u32[]{:S(2)}) collective-permute-start(bf16[64,512]{1,0:T(8,128)(2,1)S(1)} %get-tuple-element.68), channel_id=1, source_target_pairs={{0,4},{4,8},{8,12},{12,16},{16,20},{20,24},{24,28},{1,5},{5,9},{9,... | collective-permute-start | bytes 196616 | tf_op jit(solution)/shard_map/ppermute | solution.py:17
  105.9 7.3 %collective-permute-start.3 = (bf16[64,512]{1,0:T(8,128)(2,1)S(1)}, bf16[64,512]{1,0:T(8,128)(2,1)}, u32[]{:S(2)}, u32[]{:S(2)}) collective-permute-start(bf16[64,512]{1,0:T(8,128)(2,1)S(1)} %get-tuple-element.69), channel_id=1, source_target_pairs={{4,0},{8,4},{12,8},{16,12},{20,16},{24,20},{28,24},{5,1},{9,5},{13... | collective-permute-start | bytes 196616 | tf_op jit(solution)/shard_map/ppermute | solution.py:18
  116.8 20.2 %copy-start.24 = (pred[64,6]{0,1:T(8,128)(4,1)S(1)}, pred[64,6]{0,1:T(8,128)(4,1)}, u32[]{:S(2)}) copy-start(pred[64,6]{0,1:T(8,128)(4,1)} %get-tuple-element.58) | copy-start | bytes 1156
  116.8 20.9 %copy-start.4 = (bf16[384,512]{1,0:T(8,128)(2,1)S(1)}, bf16[384,512]{1,0:T(8,128)(2,1)}, u32[]{:S(2)}) copy-start(bf16[384,512]{1,0:T(8,128)(2,1)} %gather_fusion.1) | copy-start | bytes 1179652
  123.1 7.3 %collective-permute-start.4 = (bf16[64,512]{1,0:T(8,128)(2,1)S(1)}, bf16[64,512]{1,0:T(8,128)(2,1)S(1)}, u32[]{:S(2)}, u32[]{:S(2)}) collective-permute-start(bf16[64,512]{1,0:T(8,128)(2,1)S(1)} %get-tuple-element.67), channel_id=1, source_target_pairs={{0,4},{4,8},{8,12},{12,16},{16,20},{20,24},{24,28},{1,5},{5,9},{9,... | collective-permute-start | bytes 196616 | tf_op jit(solution)/shard_map/ppermute | solution.py:26
  129.1 7.1 %collective-permute-start.5 = (bf16[64,512]{1,0:T(8,128)(2,1)S(1)}, bf16[64,512]{1,0:T(8,128)(2,1)S(1)}, u32[]{:S(2)}, u32[]{:S(2)}) collective-permute-start(bf16[64,512]{1,0:T(8,128)(2,1)S(1)} %get-tuple-element.66), channel_id=1, source_target_pairs={{4,0},{8,4},{12,8},{16,12},{20,16},{24,20},{28,24},{5,1},{9,5},{13... | collective-permute-start | bytes 196616 | tf_op jit(solution)/shard_map/ppermute | solution.py:26
  137.0 120.2 %reduce-scatter.5.cloned.1.call-start = ((), (), s32[]{:S(2)}) async-start(), calls=%async_computation.4 | async-start | bytes 2621440 | tf_op jit(solution)/shard_map/reduce_scatter | solution.py:68
  138.7 25.6 %copy-start.19 = (f32[2560]{0:T(1024)S(1)}, f32[2560]{0:T(1024)}, u32[]{:S(2)}) copy-start(f32[2560]{0:T(1024)} %copy-done.18) | copy-start | bytes 30724
  196.9 26.0 %copy-start.2 = (f32[3072,512]{1,0:T(8,128)S(1)}, f32[3072,512]{1,0:T(8,128)}, u32[]{:S(2)}) copy-start(f32[3072,512]{1,0:T(8,128)} %scatter_custom_fusion.1) | copy-start | bytes 18874372
  196.9 26.0 %slice-start = ((f32[3072,512]{1,0:T(8,128)}), f32[2048,512]{1,0:T(8,128)S(1)}, s32[]{:S(2)}) async-start(f32[3072,512]{1,0:T(8,128)} %scatter_custom_fusion.1), calls=%async_computation.7 | async-start | bytes 8388608 | tf_op jit(solution)/shard_map/slice | solution.py:59
  197.0 25.9 %collective-permute-start.6 = (bf16[512,512]{1,0:T(8,128)(2,1)S(1)}, bf16[512,512]{1,0:T(8,128)(2,1)S(1)}, u32[]{:S(2)}, u32[]{:S(2)}) collective-permute-start(bf16[512,512]{1,0:T(8,128)(2,1)S(1)} %get-tuple-element.61), channel_id=1, source_target_pairs={{0,4},{4,8},{8,12},{12,16},{16,20},{20,24},{24,28},{1,5},{5,9},{9,... | collective-permute-start | bytes 1572872 | tf_op jit(solution)/shard_map/ppermute | solution.py:26
  200.7 22.4 %collective-permute-start.7 = (bf16[512,512]{1,0:T(8,128)(2,1)S(1)}, bf16[512,512]{1,0:T(8,128)(2,1)S(1)}, u32[]{:S(2)}, u32[]{:S(2)}) collective-permute-start(bf16[512,512]{1,0:T(8,128)(2,1)S(1)} %get-tuple-element.60), channel_id=1, source_target_pairs={{4,0},{8,4},{12,8},{16,12},{20,16},{24,20},{28,24},{5,1},{9,5},{13... | collective-permute-start | bytes 1572872 | tf_op jit(solution)/shard_map/ppermute | solution.py:26
  225.0 86.6 %all-reduce.7.cloned.1.call-start = ((), (), s32[]{:S(2)}) async-start(), calls=%async_computation.6 | async-start | bytes 4194304 | tf_op jit(solution)/shard_map/psum | solution.py:94
  229.5 82.1 %copy-start.11 = (bf16[64,512]{1,0:T(8,128)(2,1)S(1)}, bf16[64,512]{1,0:T(8,128)(2,1)}, u32[]{:S(2)}) copy-start(bf16[64,512]{1,0:T(8,128)(2,1)} %copy-done.10) | copy-start | bytes 196612
  229.5 82.1 %copy-start.12 = (f32[64,512]{1,0:T(8,128)S(1)}, f32[64,512]{1,0:T(8,128)}, u32[]{:S(2)}) copy-start(f32[64,512]{1,0:T(8,128)} %get-tuple-element.53) | copy-start | bytes 393220
  229.5 82.8 %copy-start.9 = (f32[512,512]{1,0:T(8,128)S(1)}, f32[512,512]{1,0:T(8,128)}, u32[]{:S(2)}) copy-start(f32[512,512]{1,0:T(8,128)} %copy-done.8) | copy-start | bytes 3145732
  229.5 82.8 %copy-start.17 = (bf16[227,512]{1,0:T(8,128)(2,1)S(1)}, bf16[227,512]{1,0:T(8,128)(2,1)}, u32[]{:S(2)}) copy-start(bf16[227,512]{1,0:T(8,128)(2,1)} %param.21) | copy-start | bytes 697348
  229.5 82.8 %copy-start.26 = (bf16[512,512]{1,0:T(8,128)(2,1)S(1)}, bf16[512,512]{1,0:T(8,128)(2,1)}, u32[]{:S(2)}) copy-start(bf16[512,512]{1,0:T(8,128)(2,1)} %param.22) | copy-start | bytes 1572868
  257.2 55.2 %copy-start.27 = (bf16[512,512]{1,0:T(8,128)(2,1)S(1)}, bf16[512,512]{1,0:T(8,128)(2,1)}, u32[]{:S(2)}) copy-start(bf16[512,512]{1,0:T(8,128)(2,1)} %reduce-scatter.5.cloned.1.call-done) | copy-start | bytes 1572868
  260.1 157.5 %all-reduce.5.cloned.1.call-start = ((), (), s32[]{:S(2)}) async-start(), calls=%async_computation.5 | async-start | bytes 4194304 | tf_op jit(solution)/shard_map/psum | solution.py:94
  (10 other events, 23.8 us)
Sparse Core Ops, SparseCore 0:
  12.2 25.2 all-gather.1
  137.1 20.5 reduce-scatter.2
  225.1 31.9 reduce-scatter.4
  260.2 51.4 all-reduce.6
  315.2 102.3 all-reduce.4
